TPU v7x, 32 devices: a whole 2x2x4 slice. The times are simulated.
32 devices in a mesh: section: 4 (over z), gx: 2 (over x), gy: 2 (over y), gz: 2 (over core).
Axes of the slice: x: 2, y: 2, z: 4, core: 2. Of those that a mesh axis runs over, the one named last changes fastest.
Arguments:
- micro_inputs: bfloat16 [1, 256, 8192], P(None, 'gy', ('gx', 'gz')), may hold values from -40 to 40
- norm_gain: float32 [4, 8192], P('section', 'gx'), may hold values from 0.5 to 1.5
- q_weight: bfloat16 [4, 8192, 8192], P('section', ('gx', 'gy'), 'gz'), may hold values from -0.0625 to 0.0625
- kv_weight: bfloat16 [4, 2, 8192, 1024], P('section', None, ('gx', 'gy'), 'gz'), may hold values from -0.0625 to 0.0625
- q_bias: float32 [4, 8192], P('section', 'gz'), may hold values from -130 to 130
- kv_bias: float32 [4, 2, 1024], P('section', None, 'gz'), may hold values from -50 to 50
- out_weight: bfloat16 [4, 8192, 8192], P('section', 'gz', ('gx', 'gy')), may hold values from -0.0625 to 0.0625
Outputs:
- hidden_out: bfloat16 [4, 1, 256, 8192], P('section', None, 'gy', ('gx', 'gz'))
All inputs are finite; a program needn't handle non-finite values.
Results may differ from a plain program's by a relative error of at most 0.025.
Values may be sent and summed in bfloat16 or wider, within the bound.
No kernel may reach another device: no remote copies, remote signals or barrier semaphores. Data moves between devices by JAX's collectives and lax.ppermute only.
A program may use at most 128 MiB of HBM per device.

v0:
```python
import jax
import jax.numpy as jnp
from jax import lax
from jax.sharding import PartitionSpec as P

D = 8192
HD = 128
ROPE_BASE = 1000000.0
EPSILON = 1e-06
NEG_FILL = -1e30


def from_behind(value, axis, steps):
    count = lax.axis_size(axis)
    initial, last = (max(0, -steps), min(count, count - steps))
    return lax.ppermute(value, axis, [(source, source + steps) for source in range(initial, last)])


def rotary(values, positions):
    half_width = values.shape[-1] // 2
    frequency = ROPE_BASE ** (-jnp.arange(half_width, dtype=jnp.float32) * 2.0 / values.shape[-1])
    angles = positions.astype(jnp.float32)[:, None] * frequency[None, :]
    cosine = jnp.cos(angles)[:, None, :]
    sine_part = jnp.sin(angles)[:, None, :]
    lower_half = values[..., :half_width]
    upper_half = values[..., half_width:]
    return jnp.concatenate(
        [
            lower_half * cosine - upper_half * sine_part,
            upper_half * cosine + lower_half * sine_part,
        ],
        axis=-1,
    )


def body(micro_inputs, norm_gain, q_weight, kv_weight, q_bias, kv_bias, out_weight):
    section_count = lax.axis_size("section")
    size_gx = lax.axis_size("gx")
    micro_count = micro_inputs.shape[0]
    local_rows = micro_inputs.shape[1]
    index_gx = lax.axis_index("gx")
    index_gy = lax.axis_index("gy")
    index_section = lax.axis_index("section")
    query_weight = q_weight[0]
    pair_weight = jnp.concatenate([kv_weight[0, 0], kv_weight[0, 1]], axis=1)
    mixing_weight = out_weight[0]
    slab_rows = q_weight.shape[1]
    q_cols = query_weight.shape[1]
    kv_cols = pair_weight.shape[1] // 2
    gain_row = norm_gain[0]
    q_heads = q_cols // HD
    kv_heads = kv_cols // HD
    group_size = q_heads // kv_heads
    own_cols = q_cols // size_gx
    own_heads = own_cols // HD
    if own_heads > group_size:
        used_heads = own_heads // group_size
        local_group = group_size
    else:
        used_heads = 1
        local_group = own_heads
    used_start = index_gx * own_heads // group_size
    score_scale = HD ** (-0.5)
    row_pos = index_gy * local_rows + jnp.arange(local_rows)
    own_bias = lax.dynamic_slice_in_dim(q_bias[0], index_gx * own_cols, own_cols, 0)

    def mix_cols(piece):
        return jnp.dot(piece, mixing_weight, preferred_element_type=jnp.float32)

    def attention_layer(wide_block):
        widened = wide_block.astype(jnp.float32)
        squares = lax.psum(jnp.sum(widened * widened, axis=1), "gx")
        normed = (widened * lax.rsqrt(squares / D + EPSILON)[:, None] * gain_row[None, :]).astype(
            jnp.bfloat16
        )
        all_tokens = lax.all_gather(normed, "gy", axis=0, tiled=True)
        own_slab = lax.dynamic_slice_in_dim(all_tokens, index_gy * slab_rows, slab_rows, 1)
        query_part = jnp.dot(own_slab, query_weight, preferred_element_type=jnp.float32)
        pair_part = jnp.dot(own_slab, pair_weight, preferred_element_type=jnp.float32)
        query_rows, pair_local = (
            lax.psum_scatter(
                query_part.astype(jnp.bfloat16), "gy", scatter_dimension=0, tiled=True
            ).astype(jnp.float32),
            lax.psum_scatter(
                pair_part.astype(jnp.bfloat16), "gy", scatter_dimension=0, tiled=True
            ).astype(jnp.float32),
        )
        queries = (
            lax.psum_scatter(
                query_rows.astype(jnp.bfloat16), "gx", scatter_dimension=1, tiled=True
            ).astype(jnp.float32)
            + own_bias[None, :]
        )
        pair_terms = lax.psum(pair_local.astype(jnp.bfloat16), "gx").astype(jnp.float32)
        key_rows = pair_terms[:, :kv_cols] + kv_bias[0, 0][None, :]
        value_rows = (pair_terms[:, kv_cols:] + kv_bias[0, 1][None, :]).astype(jnp.bfloat16)
        queries = rotary(queries.reshape(local_rows, own_heads, HD), row_pos).astype(jnp.bfloat16)
        queries = queries.reshape(local_rows, used_heads, local_group, HD)
        key_rows = rotary(key_rows.reshape(local_rows, kv_heads, HD), row_pos).astype(jnp.bfloat16)
        key_used = lax.dynamic_slice_in_dim(key_rows, used_start, used_heads, 1).reshape(
            local_rows, used_heads * HD
        )
        value_used = lax.dynamic_slice_in_dim(
            value_rows.reshape(local_rows, kv_heads, HD), used_start, used_heads, 1
        ).reshape(local_rows, used_heads * HD)
        running_max = jnp.full((used_heads, local_group, local_rows), NEG_FILL, jnp.float32)
        key_piece = lax.all_gather(key_used, "gy", axis=0, tiled=True)
        value_piece = lax.all_gather(value_used, "gy", axis=0, tiled=True)
        key_count = key_piece.shape[0]
        key_pos = jnp.arange(key_count)
        scores = (
            jnp.einsum(
                "qhgd,khd->hgqk",
                queries,
                key_piece.reshape(key_count, used_heads, HD),
                preferred_element_type=jnp.float32,
            )
            * score_scale
        )
        allowed = key_pos[None, :] <= row_pos[:, None]
        scores = jnp.where(allowed, scores, NEG_FILL)
        new_max = jnp.maximum(running_max, jnp.max(scores, axis=-1))
        weights = jnp.where(allowed, jnp.exp(scores - new_max[..., None]), 0.0)
        running_sum = jnp.sum(weights, axis=-1)
        update = jnp.einsum(
            "hgqk,khd->qhgd",
            weights.astype(jnp.bfloat16),
            value_piece.reshape(key_count, used_heads, HD),
            preferred_element_type=jnp.float32,
        )
        weighted = update
        running_max, running_sum, weighted = (new_max, running_sum, weighted)
        attended = (
            (weighted / jnp.transpose(running_sum, (2, 0, 1))[..., None])
            .astype(jnp.bfloat16)
            .reshape(local_rows, own_cols)
        )
        every_token = lax.all_gather(attended, "gy", axis=0, tiled=True)
        column_sums = mix_cols(lax.all_gather(every_token, "gx", axis=1, tiled=True))
        return lax.all_to_all(
            column_sums.astype(jnp.bfloat16), "gy", split_axis=0, concat_axis=1, tiled=True
        ).astype(column_sums.dtype)

    def record(stored, tick_index, result):
        micro_index = tick_index - index_section
        is_valid = (micro_index >= 0) & (micro_index < micro_count)
        clipped = jnp.clip(micro_index, 0, micro_count - 1)
        previous = lax.dynamic_index_in_dim(stored, clipped, 0, keepdims=False)
        return lax.dynamic_update_index_in_dim(
            stored, jnp.where(is_valid, result, previous), clipped, 0
        )

    tick_count = micro_count + section_count - 1
    stored_start = jnp.zeros(micro_inputs.shape, jnp.bfloat16)

    def advance(tick_index, state):
        carried, stored = state
        fresh = lax.dynamic_index_in_dim(
            micro_inputs, jnp.clip(tick_index, 0, micro_count - 1), 0, keepdims=False
        )
        current = jnp.where(index_section == 0, fresh, carried)
        wide_block = lax.all_gather(current, "gz", axis=1, tiled=True)
        summed = lax.psum_scatter(
            attention_layer(wide_block).astype(jnp.bfloat16), "gz", scatter_dimension=1, tiled=True
        ).astype(jnp.float32)
        result = (current.astype(jnp.float32) + summed).astype(jnp.bfloat16)
        stored = record(stored, tick_index, result)
        return (from_behind(result, "section", 1), stored)

    carry_start = jnp.zeros(micro_inputs.shape[1:], jnp.bfloat16)
    final_state = lax.fori_loop(0, tick_count, advance, (carry_start, stored_start))
    return final_state[1][None]


def solution(mesh):
    return jax.shard_map(
        body,
        mesh=mesh,
        in_specs=(
            P(None, "gy", ("gx", "gz")),
            P("section", "gx"),
            P("section", ("gx", "gy"), "gz"),
            P("section", None, ("gx", "gy"), "gz"),
            P("section", "gz"),
            P("section", None, "gz"),
            P("section", "gz", ("gx", "gy")),
        ),
        out_specs=P("section", None, "gy", ("gx", "gz")),
        check_vma=False,
    )
```

profile of v0, /device:TPU:0, one launch (start us, length us, event | category | flops | bytes accessed | tf_op | source)
XLA Modules:
  0.0 1107.2 jit_solution(5537659410085549743)
XLA Ops:
  12.5 1087.3 %while.19 = (s32[]{:T(128)}, bf16[128,2048]{1,0:T(8,128)(2,1)S(1)}, bf16[1,128,2048]{2,1,0:T(8,128)(2,1)S(1)}, pred[]{:T(512)}, bf16[1,128,2048]{2,1,0:T(8,128)(...) while((s32[]{:T(128)}, bf16[128,2048]{1,0:T(8,128)(2,1)S(1)}, ...), condition=%wide.region_10.11_spmd.clone.clone, body=%wide.region_0.10_spmd.clone.clone.sunk | while | flops 9950043136 | bytes 130518144 | solution.py:171
  13.5 13.2 %all-gather.5.cloned.1.call-done = bf16[128,4096]{1,0:T(8,128)(2,1)} async-done(((bf16[128,2048]{1,0:T(8,128)(2,1)}), bf16[128,4096]{1,0:T(8,128)(2,1)}) %all-gather.5.cloned.1.call-update) | async-done | bytes 1048592 | tf_op jit(solution)/shard_map/while/body/eval_jaxpr/all_gather | solution.py:162
  28.2 4.9 psum.34
  35.8 34.4 %all-gather.7.cloned.1.call-done = bf16[256,4096]{1,0:T(8,128)(2,1)} async-done(((bf16[128,4096]{1,0:T(8,128)(2,1)}), bf16[256,4096]{1,0:T(8,128)(2,1)}) %all-gather.7.cloned.1.call-update) | async-done | bytes 2097168 | tf_op jit(solution)/shard_map/while/body/eval_jaxpr/all_gather | solution.py:76
  70.2 4.6 convolution_convert_fusion.6
  74.8 12.0 %convolution_convert_fusion.7 = bf16[256,4096]{1,0:T(8,128)(2,1)} fusion(bf16[2048,4096]{1,0:T(8,128)(2,1)} %get-tuple-element.638, bf16[256,4096]{1,0:T(8,128)(2,1)} %all-gather.7.cloned.1.call-done, s32[]{:T(128)} %get-tuple-element.634), kind=kOutput, calls=%fused_computation.2.clone.1 | convolution fusion | flops 4296015872 | bytes 19923456 | tf_op jit(solution)/shard_map/while/body/eval_jaxpr/dot_general | solution.py:78
  89.7 34.0 %reduce-scatter.7.cloned.1.call-done = bf16[128,4096]{1,0:T(8,128)(2,1)} async-done(((bf16[256,4096]{1,0:T(8,128)(2,1)}), bf16[128,4096]{1,0:T(8,128)(2,1)}) %reduce-scatter.7.cloned.1.call-update) | async-done | bytes 1048592 | tf_op jit(solution)/shard_map/while/body/eval_jaxpr/reduce_scatter | solution.py:81
  124.1 25.0 %all-reduce.2.cloned.1.call-done = bf16[128,1024]{1,0:T(8,128)(2,1)} async-done(((bf16[128,1024]{1,0:T(8,128)(2,1)}), bf16[128,1024]{1,0:T(8,128)(2,1)}) %all-reduce.2.cloned.1.call-update) | async-done | bytes 262160 | tf_op jit(solution)/shard_map/while/body/eval_jaxpr/psum | solution.py:94
  151.0 5.0 all_gather.81
  156.0 5.0 all_gather.80
  161.0 10.6 reduce-scatter.9.cloned.1.call-done
  176.5 21.4 %all-gather.9.cloned.1.call-done = bf16[256,2048]{0,1:T(8,128)(2,1)} async-done(((bf16[128,2048]{0,1:T(8,128)(2,1)}), bf16[256,2048]{0,1:T(8,128)(2,1)}) %all-gather.9.cloned.1.call-update) | async-done | bytes 1048592 | tf_op jit(solution)/shard_map/while/body/eval_jaxpr/all_gather | solution.py:138
  197.9 34.6 %all-gather.11.cloned.1.call-done = bf16[256,4096]{0,1:T(8,128)(2,1)} async-done(((bf16[256,2048]{0,1:T(8,128)(2,1)}), bf16[256,4096]{0,1:T(8,128)(2,1)}) %all-gather.11.cloned.1.call-update) | async-done | bytes 2097168 | tf_op jit(solution)/shard_map/while/body/eval_jaxpr/all_gather | solution.py:139
  232.5 10.9 convolution_convert_fusion.8
  243.5 16.2 %all_to_all.48 = bf16[2,128,2048]{2,1,0:T(8,128)(2,1)S(1)} all-to-all(bf16[2,128,2048]{2,1,0:T(8,128)(2,1)S(1)} %bitcast.132), channel_id=1, replica_groups=mesh['section'=4,'gx'=2,'gy'=2,'gz'=2] {'gy'}, dimensions={0} | all-to-all | bytes 2097152 | tf_op jit(solution)/shard_map/while/body/eval_jaxpr/all_to_all | solution.py:140
  260.7 7.6 reduce-scatter.11.cloned.1.call-done
  273.4 11.6 %collective-permute-done = bf16[128,2048]{1,0:T(8,128)(2,1)S(1)} collective-permute-done((bf16[128,2048]{1,0:T(8,128)(2,1)S(1)}, bf16[128,2048]{1,0:T(8,128)(2,1)S(1)}, u32[]{:S(2)}, u32[]{:S(2)}) %collective-permute-start) | collective-permute-done | bytes 524320 | tf_op jit(solution)/shard_map/while/body/eval_jaxpr/ppermute | solution.py:16
  285.9 12.1 %all-gather.5.cloned.1.call-done = bf16[128,4096]{1,0:T(8,128)(2,1)} async-done(((bf16[128,2048]{1,0:T(8,128)(2,1)}), bf16[128,4096]{1,0:T(8,128)(2,1)}) %all-gather.5.cloned.1.call-update) | async-done | bytes 1048592 | tf_op jit(solution)/shard_map/while/body/eval_jaxpr/all_gather | solution.py:162
  299.5 4.9 psum.34
  307.0 34.4 %all-gather.7.cloned.1.call-done = bf16[256,4096]{1,0:T(8,128)(2,1)} async-done(((bf16[128,4096]{1,0:T(8,128)(2,1)}), bf16[256,4096]{1,0:T(8,128)(2,1)}) %all-gather.7.cloned.1.call-update) | async-done | bytes 2097168 | tf_op jit(solution)/shard_map/while/body/eval_jaxpr/all_gather | solution.py:76
  346.1 12.0 %convolution_convert_fusion.7 = bf16[256,4096]{1,0:T(8,128)(2,1)} fusion(bf16[2048,4096]{1,0:T(8,128)(2,1)} %get-tuple-element.638, bf16[256,4096]{1,0:T(8,128)(2,1)} %all-gather.7.cloned.1.call-done, s32[]{:T(128)} %get-tuple-element.634), kind=kOutput, calls=%fused_computation.2.clone.1 | convolution fusion | flops 4296015872 | bytes 19923456 | tf_op jit(solution)/shard_map/while/body/eval_jaxpr/dot_general | solution.py:78
  360.9 34.1 %reduce-scatter.7.cloned.1.call-done = bf16[128,4096]{1,0:T(8,128)(2,1)} async-done(((bf16[256,4096]{1,0:T(8,128)(2,1)}), bf16[128,4096]{1,0:T(8,128)(2,1)}) %reduce-scatter.7.cloned.1.call-update) | async-done | bytes 1048592 | tf_op jit(solution)/shard_map/while/body/eval_jaxpr/reduce_scatter | solution.py:81
  395.5 25.0 %all-reduce.2.cloned.1.call-done = bf16[128,1024]{1,0:T(8,128)(2,1)} async-done(((bf16[128,1024]{1,0:T(8,128)(2,1)}), bf16[128,1024]{1,0:T(8,128)(2,1)}) %all-reduce.2.cloned.1.call-update) | async-done | bytes 262160 | tf_op jit(solution)/shard_map/while/body/eval_jaxpr/psum | solution.py:94
  422.5 5.0 all_gather.81
  427.4 5.0 all_gather.80
  432.4 10.6 reduce-scatter.9.cloned.1.call-done
  447.9 21.4 %all-gather.9.cloned.1.call-done = bf16[256,2048]{0,1:T(8,128)(2,1)} async-done(((bf16[128,2048]{0,1:T(8,128)(2,1)}), bf16[256,2048]{0,1:T(8,128)(2,1)}) %all-gather.9.cloned.1.call-update) | async-done | bytes 1048592 | tf_op jit(solution)/shard_map/while/body/eval_jaxpr/all_gather | solution.py:138
  469.4 34.4 %all-gather.11.cloned.1.call-done = bf16[256,4096]{0,1:T(8,128)(2,1)} async-done(((bf16[256,2048]{0,1:T(8,128)(2,1)}), bf16[256,4096]{0,1:T(8,128)(2,1)}) %all-gather.11.cloned.1.call-update) | async-done | bytes 2097168 | tf_op jit(solution)/shard_map/while/body/eval_jaxpr/all_gather | solution.py:139
  503.8 10.9 convolution_convert_fusion.8
  514.7 16.2 %all_to_all.48 = bf16[2,128,2048]{2,1,0:T(8,128)(2,1)S(1)} all-to-all(bf16[2,128,2048]{2,1,0:T(8,128)(2,1)S(1)} %bitcast.132), channel_id=1, replica_groups=mesh['section'=4,'gx'=2,'gy'=2,'gz'=2] {'gy'}, dimensions={0} | all-to-all | bytes 2097152 | tf_op jit(solution)/shard_map/while/body/eval_jaxpr/all_to_all | solution.py:140
  532.0 7.6 reduce-scatter.11.cloned.1.call-done
  544.6 11.6 %collective-permute-done = bf16[128,2048]{1,0:T(8,128)(2,1)S(1)} collective-permute-done((bf16[128,2048]{1,0:T(8,128)(2,1)S(1)}, bf16[128,2048]{1,0:T(8,128)(2,1)S(1)}, u32[]{:S(2)}, u32[]{:S(2)}) %collective-permute-start) | collective-permute-done | bytes 524320 | tf_op jit(solution)/shard_map/while/body/eval_jaxpr/ppermute | solution.py:16
  557.1 12.4 %all-gather.5.cloned.1.call-done = bf16[128,4096]{1,0:T(8,128)(2,1)} async-done(((bf16[128,2048]{1,0:T(8,128)(2,1)}), bf16[128,4096]{1,0:T(8,128)(2,1)}) %all-gather.5.cloned.1.call-update) | async-done | bytes 1048592 | tf_op jit(solution)/shard_map/while/body/eval_jaxpr/all_gather | solution.py:162
  571.1 4.9 psum.34
  578.6 34.4 %all-gather.7.cloned.1.call-done = bf16[256,4096]{1,0:T(8,128)(2,1)} async-done(((bf16[128,4096]{1,0:T(8,128)(2,1)}), bf16[256,4096]{1,0:T(8,128)(2,1)}) %all-gather.7.cloned.1.call-update) | async-done | bytes 2097168 | tf_op jit(solution)/shard_map/while/body/eval_jaxpr/all_gather | solution.py:76
  613.0 4.6 convolution_convert_fusion.6
  617.7 12.0 %convolution_convert_fusion.7 = bf16[256,4096]{1,0:T(8,128)(2,1)} fusion(bf16[2048,4096]{1,0:T(8,128)(2,1)} %get-tuple-element.638, bf16[256,4096]{1,0:T(8,128)(2,1)} %all-gather.7.cloned.1.call-done, s32[]{:T(128)} %get-tuple-element.634), kind=kOutput, calls=%fused_computation.2.clone.1 | convolution fusion | flops 4296015872 | bytes 19923456 | tf_op jit(solution)/shard_map/while/body/eval_jaxpr/dot_general | solution.py:78
  632.5 34.1 %reduce-scatter.7.cloned.1.call-done = bf16[128,4096]{1,0:T(8,128)(2,1)} async-done(((bf16[256,4096]{1,0:T(8,128)(2,1)}), bf16[128,4096]{1,0:T(8,128)(2,1)}) %reduce-scatter.7.cloned.1.call-update) | async-done | bytes 1048592 | tf_op jit(solution)/shard_map/while/body/eval_jaxpr/reduce_scatter | solution.py:81
  667.1 25.1 %all-reduce.2.cloned.1.call-done = bf16[128,1024]{1,0:T(8,128)(2,1)} async-done(((bf16[128,1024]{1,0:T(8,128)(2,1)}), bf16[128,1024]{1,0:T(8,128)(2,1)}) %all-reduce.2.cloned.1.call-update) | async-done | bytes 262160 | tf_op jit(solution)/shard_map/while/body/eval_jaxpr/psum | solution.py:94
  694.2 5.0 all_gather.81
  699.1 5.0 all_gather.80
  704.1 10.6 reduce-scatter.9.cloned.1.call-done
  719.7 21.4 %all-gather.9.cloned.1.call-done = bf16[256,2048]{0,1:T(8,128)(2,1)} async-done(((bf16[128,2048]{0,1:T(8,128)(2,1)}), bf16[256,2048]{0,1:T(8,128)(2,1)}) %all-gather.9.cloned.1.call-update) | async-done | bytes 1048592 | tf_op jit(solution)/shard_map/while/body/eval_jaxpr/all_gather | solution.py:138
  741.1 34.4 %all-gather.11.cloned.1.call-done = bf16[256,4096]{0,1:T(8,128)(2,1)} async-done(((bf16[256,2048]{0,1:T(8,128)(2,1)}), bf16[256,4096]{0,1:T(8,128)(2,1)}) %all-gather.11.cloned.1.call-update) | async-done | bytes 2097168 | tf_op jit(solution)/shard_map/while/body/eval_jaxpr/all_gather | solution.py:139
  775.5 10.9 convolution_convert_fusion.8
  786.4 16.2 %all_to_all.48 = bf16[2,128,2048]{2,1,0:T(8,128)(2,1)S(1)} all-to-all(bf16[2,128,2048]{2,1,0:T(8,128)(2,1)S(1)} %bitcast.132), channel_id=1, replica_groups=mesh['section'=4,'gx'=2,'gy'=2,'gz'=2] {'gy'}, dimensions={0} | all-to-all | bytes 2097152 | tf_op jit(solution)/shard_map/while/body/eval_jaxpr/all_to_all | solution.py:140
  803.7 7.6 reduce-scatter.11.cloned.1.call-done
  816.4 11.6 %collective-permute-done = bf16[128,2048]{1,0:T(8,128)(2,1)S(1)} collective-permute-done((bf16[128,2048]{1,0:T(8,128)(2,1)S(1)}, bf16[128,2048]{1,0:T(8,128)(2,1)S(1)}, u32[]{:S(2)}, u32[]{:S(2)}) %collective-permute-start) | collective-permute-done | bytes 524320 | tf_op jit(solution)/shard_map/while/body/eval_jaxpr/ppermute | solution.py:16
  828.9 12.4 %all-gather.5.cloned.1.call-done = bf16[128,4096]{1,0:T(8,128)(2,1)} async-done(((bf16[128,2048]{1,0:T(8,128)(2,1)}), bf16[128,4096]{1,0:T(8,128)(2,1)}) %all-gather.5.cloned.1.call-update) | async-done | bytes 1048592 | tf_op jit(solution)/shard_map/while/body/eval_jaxpr/all_gather | solution.py:162
  842.8 4.9 psum.34
  850.4 34.4 %all-gather.7.cloned.1.call-done = bf16[256,4096]{1,0:T(8,128)(2,1)} async-done(((bf16[128,4096]{1,0:T(8,128)(2,1)}), bf16[256,4096]{1,0:T(8,128)(2,1)}) %all-gather.7.cloned.1.call-update) | async-done | bytes 2097168 | tf_op jit(solution)/shard_map/while/body/eval_jaxpr/all_gather | solution.py:76
  884.7 4.6 convolution_convert_fusion.6
  889.4 12.0 %convolution_convert_fusion.7 = bf16[256,4096]{1,0:T(8,128)(2,1)} fusion(bf16[2048,4096]{1,0:T(8,128)(2,1)} %get-tuple-element.638, bf16[256,4096]{1,0:T(8,128)(2,1)} %all-gather.7.cloned.1.call-done, s32[]{:T(128)} %get-tuple-element.634), kind=kOutput, calls=%fused_computation.2.clone.1 | convolution fusion | flops 4296015872 | bytes 19923456 | tf_op jit(solution)/shard_map/while/body/eval_jaxpr/dot_general | solution.py:78
  904.2 34.1 %reduce-scatter.7.cloned.1.call-done = bf16[128,4096]{1,0:T(8,128)(2,1)} async-done(((bf16[256,4096]{1,0:T(8,128)(2,1)}), bf16[128,4096]{1,0:T(8,128)(2,1)}) %reduce-scatter.7.cloned.1.call-update) | async-done | bytes 1048592 | tf_op jit(solution)/shard_map/while/body/eval_jaxpr/reduce_scatter | solution.py:81
  938.8 25.1 %all-reduce.2.cloned.1.call-done = bf16[128,1024]{1,0:T(8,128)(2,1)} async-done(((bf16[128,1024]{1,0:T(8,128)(2,1)}), bf16[128,1024]{1,0:T(8,128)(2,1)}) %all-reduce.2.cloned.1.call-update) | async-done | bytes 262160 | tf_op jit(solution)/shard_map/while/body/eval_jaxpr/psum | solution.py:94
  965.9 5.0 all_gather.81
  970.9 5.0 all_gather.80
  975.9 10.6 reduce-scatter.9.cloned.1.call-done
  991.4 21.4 %all-gather.9.cloned.1.call-done = bf16[256,2048]{0,1:T(8,128)(2,1)} async-done(((bf16[128,2048]{0,1:T(8,128)(2,1)}), bf16[256,2048]{0,1:T(8,128)(2,1)}) %all-gather.9.cloned.1.call-update) | async-done | bytes 1048592 | tf_op jit(solution)/shard_map/while/body/eval_jaxpr/all_gather | solution.py:138
  1012.8 34.6 %all-gather.11.cloned.1.call-done = bf16[256,4096]{0,1:T(8,128)(2,1)} async-done(((bf16[256,2048]{0,1:T(8,128)(2,1)}), bf16[256,4096]{0,1:T(8,128)(2,1)}) %all-gather.11.cloned.1.call-update) | async-done | bytes 2097168 | tf_op jit(solution)/shard_map/while/body/eval_jaxpr/all_gather | solution.py:139
  1047.4 10.9 convolution_convert_fusion.8
  1058.3 16.2 %all_to_all.48 = bf16[2,128,2048]{2,1,0:T(8,128)(2,1)S(1)} all-to-all(bf16[2,128,2048]{2,1,0:T(8,128)(2,1)S(1)} %bitcast.132), channel_id=1, replica_groups=mesh['section'=4,'gx'=2,'gy'=2,'gz'=2] {'gy'}, dimensions={0} | all-to-all | bytes 2097152 | tf_op jit(solution)/shard_map/while/body/eval_jaxpr/all_to_all | solution.py:140
  1075.6 7.6 reduce-scatter.11.cloned.1.call-done
  1088.3 11.6 %collective-permute-done = bf16[128,2048]{1,0:T(8,128)(2,1)S(1)} collective-permute-done((bf16[128,2048]{1,0:T(8,128)(2,1)S(1)}, bf16[128,2048]{1,0:T(8,128)(2,1)S(1)}, u32[]{:S(2)}, u32[]{:S(2)}) %collective-permute-start) | collective-permute-done | bytes 524320 | tf_op jit(solution)/shard_map/while/body/eval_jaxpr/ppermute | solution.py:16
  (222 shorter events, 96.5 us)
Async XLA Ops:
  6.5 0.7 copy-start
  9.8 2.8 copy-start.4
  9.8 2.8 copy-start.5
  9.8 2.8 copy-start.6
  12.6 14.1 %all-gather.5.cloned.1.call-start = ((), (), s32[]{:S(2)}) async-start(), calls=%async_computation.5 | async-start | bytes 1572864 | tf_op jit(solution)/shard_map/while/body/eval_jaxpr/all_gather | solution.py:162
  13.5 56.7 %all-gather.7.cloned.1.call-start = ((), (), s32[]{:S(2)}) async-start(), calls=%async_computation.6 | async-start | bytes 3145728 | tf_op jit(solution)/shard_map/while/body/eval_jaxpr/all_gather | solution.py:76
  35.7 53.9 %reduce-scatter.5.cloned.1.call-start = ((), (), s32[]{:S(2)}) async-start(), calls=%async_computation.7 | async-start | bytes 786432 | tf_op jit(solution)/shard_map/while/body/eval_jaxpr/reduce_scatter | solution.py:84
  74.8 48.8 %reduce-scatter.7.cloned.1.call-start = ((), (), s32[]{:S(2)}) async-start(), calls=%async_computation.9 | async-start | bytes 3145728 | tf_op jit(solution)/shard_map/while/body/eval_jaxpr/reduce_scatter | solution.py:81
  86.8 62.2 %all-reduce.2.cloned.1.call-start = ((), (), s32[]{:S(2)}) async-start(), calls=%async_computation.8 | async-start | bytes 524288 | tf_op jit(solution)/shard_map/while/body/eval_jaxpr/psum | solution.py:94
  89.6 82.0 %reduce-scatter.9.cloned.1.call-start = ((), (), s32[]{:S(2)}) async-start(), calls=%async_computation.10 | async-start | bytes 1572864 | tf_op jit(solution)/shard_map/while/body/eval_jaxpr/reduce_scatter | solution.py:89
  123.7 74.2 %all-gather.9.cloned.1.call-start = ((), (), s32[]{:S(2)}) async-start(), calls=%async_computation.11 | async-start | bytes 1572864 | tf_op jit(solution)/shard_map/while/body/eval_jaxpr/all_gather | solution.py:138
  176.5 56.1 %all-gather.11.cloned.1.call-start = ((), (), s32[]{:S(2)}) async-start(), calls=%async_computation.12 | async-start | bytes 3145728 | tf_op jit(solution)/shard_map/while/body/eval_jaxpr/all_gather | solution.py:139
  197.9 70.4 %reduce-scatter.11.cloned.1.call-start = ((), (), s32[]{:S(2)}) async-start(), calls=%async_computation.13 | async-start | bytes 1572864 | tf_op jit(solution)/shard_map/while/body/eval_jaxpr/reduce_scatter | solution.py:163
  259.6 8.7 copy-start.2
  269.7 15.3 %collective-permute-start = (bf16[128,2048]{1,0:T(8,128)(2,1)S(1)}, bf16[128,2048]{1,0:T(8,128)(2,1)S(1)}, u32[]{:S(2)}, u32[]{:S(2)}) collective-permute-start(bf16[128,2048]{1,0:T(8,128)(2,1)S(1)} %get-tuple-element.592), channel_id=1, source_target_pairs={{0,8},{8,16},{16,24},{1,9},{9,17},{17,25},{2,10},{10,18},{18,26},{... | collective-permute-start | bytes 1572872 | tf_op jit(solution)/shard_map/while/body/eval_jaxpr/ppermute | solution.py:16
  285.0 13.0 %all-gather.5.cloned.1.call-start = ((), (), s32[]{:S(2)}) async-start(), calls=%async_computation.5 | async-start | bytes 1572864 | tf_op jit(solution)/shard_map/while/body/eval_jaxpr/all_gather | solution.py:162
  285.8 55.6 %all-gather.7.cloned.1.call-start = ((), (), s32[]{:S(2)}) async-start(), calls=%async_computation.6 | async-start | bytes 3145728 | tf_op jit(solution)/shard_map/while/body/eval_jaxpr/all_gather | solution.py:76
  307.0 53.9 %reduce-scatter.5.cloned.1.call-start = ((), (), s32[]{:S(2)}) async-start(), calls=%async_computation.7 | async-start | bytes 786432 | tf_op jit(solution)/shard_map/while/body/eval_jaxpr/reduce_scatter | solution.py:84
  346.1 49.0 %reduce-scatter.7.cloned.1.call-start = ((), (), s32[]{:S(2)}) async-start(), calls=%async_computation.9 | async-start | bytes 3145728 | tf_op jit(solution)/shard_map/while/body/eval_jaxpr/reduce_scatter | solution.py:81
  358.1 62.4 %all-reduce.2.cloned.1.call-start = ((), (), s32[]{:S(2)}) async-start(), calls=%async_computation.8 | async-start | bytes 524288 | tf_op jit(solution)/shard_map/while/body/eval_jaxpr/psum | solution.py:94
  360.9 82.1 %reduce-scatter.9.cloned.1.call-start = ((), (), s32[]{:S(2)}) async-start(), calls=%async_computation.10 | async-start | bytes 1572864 | tf_op jit(solution)/shard_map/while/body/eval_jaxpr/reduce_scatter | solution.py:89
  395.1 74.2 %all-gather.9.cloned.1.call-start = ((), (), s32[]{:S(2)}) async-start(), calls=%async_computation.11 | async-start | bytes 1572864 | tf_op jit(solution)/shard_map/while/body/eval_jaxpr/all_gather | solution.py:138
  447.9 55.9 %all-gather.11.cloned.1.call-start = ((), (), s32[]{:S(2)}) async-start(), calls=%async_computation.12 | async-start | bytes 3145728 | tf_op jit(solution)/shard_map/while/body/eval_jaxpr/all_gather | solution.py:139
  469.3 70.3 %reduce-scatter.11.cloned.1.call-start = ((), (), s32[]{:S(2)}) async-start(), calls=%async_computation.13 | async-start | bytes 1572864 | tf_op jit(solution)/shard_map/while/body/eval_jaxpr/reduce_scatter | solution.py:163
  530.9 8.7 copy-start.2
  540.9 15.3 %collective-permute-start = (bf16[128,2048]{1,0:T(8,128)(2,1)S(1)}, bf16[128,2048]{1,0:T(8,128)(2,1)S(1)}, u32[]{:S(2)}, u32[]{:S(2)}) collective-permute-start(bf16[128,2048]{1,0:T(8,128)(2,1)S(1)} %get-tuple-element.592), channel_id=1, source_target_pairs={{0,8},{8,16},{16,24},{1,9},{9,17},{17,25},{2,10},{10,18},{18,26},{... | collective-permute-start | bytes 1572872 | tf_op jit(solution)/shard_map/while/body/eval_jaxpr/ppermute | solution.py:16
  556.2 13.3 %all-gather.5.cloned.1.call-start = ((), (), s32[]{:S(2)}) async-start(), calls=%async_computation.5 | async-start | bytes 1572864 | tf_op jit(solution)/shard_map/while/body/eval_jaxpr/all_gather | solution.py:162
  557.1 55.9 %all-gather.7.cloned.1.call-start = ((), (), s32[]{:S(2)}) async-start(), calls=%async_computation.6 | async-start | bytes 3145728 | tf_op jit(solution)/shard_map/while/body/eval_jaxpr/all_gather | solution.py:76
  578.6 53.9 %reduce-scatter.5.cloned.1.call-start = ((), (), s32[]{:S(2)}) async-start(), calls=%async_computation.7 | async-start | bytes 786432 | tf_op jit(solution)/shard_map/while/body/eval_jaxpr/reduce_scatter | solution.py:84
  617.6 49.0 %reduce-scatter.7.cloned.1.call-start = ((), (), s32[]{:S(2)}) async-start(), calls=%async_computation.9 | async-start | bytes 3145728 | tf_op jit(solution)/shard_map/while/body/eval_jaxpr/reduce_scatter | solution.py:81
  629.7 62.5 %all-reduce.2.cloned.1.call-start = ((), (), s32[]{:S(2)}) async-start(), calls=%async_computation.8 | async-start | bytes 524288 | tf_op jit(solution)/shard_map/while/body/eval_jaxpr/psum | solution.py:94
  632.5 82.3 %reduce-scatter.9.cloned.1.call-start = ((), (), s32[]{:S(2)}) async-start(), calls=%async_computation.10 | async-start | bytes 1572864 | tf_op jit(solution)/shard_map/while/body/eval_jaxpr/reduce_scatter | solution.py:89
  666.6 74.4 %all-gather.9.cloned.1.call-start = ((), (), s32[]{:S(2)}) async-start(), calls=%async_computation.11 | async-start | bytes 1572864 | tf_op jit(solution)/shard_map/while/body/eval_jaxpr/all_gather | solution.py:138
  719.6 55.9 %all-gather.11.cloned.1.call-start = ((), (), s32[]{:S(2)}) async-start(), calls=%async_computation.12 | async-start | bytes 3145728 | tf_op jit(solution)/shard_map/while/body/eval_jaxpr/all_gather | solution.py:139
  741.0 70.3 %reduce-scatter.11.cloned.1.call-start = ((), (), s32[]{:S(2)}) async-start(), calls=%async_computation.13 | async-start | bytes 1572864 | tf_op jit(solution)/shard_map/while/body/eval_jaxpr/reduce_scatter | solution.py:163
  802.6 8.7 copy-start.2
  812.7 15.3 %collective-permute-start = (bf16[128,2048]{1,0:T(8,128)(2,1)S(1)}, bf16[128,2048]{1,0:T(8,128)(2,1)S(1)}, u32[]{:S(2)}, u32[]{:S(2)}) collective-permute-start(bf16[128,2048]{1,0:T(8,128)(2,1)S(1)} %get-tuple-element.592), channel_id=1, source_target_pairs={{0,8},{8,16},{16,24},{1,9},{9,17},{17,25},{2,10},{10,18},{18,26},{... | collective-permute-start | bytes 1572872 | tf_op jit(solution)/shard_map/while/body/eval_jaxpr/ppermute | solution.py:16
  827.9 13.3 %all-gather.5.cloned.1.call-start = ((), (), s32[]{:S(2)}) async-start(), calls=%async_computation.5 | async-start | bytes 1572864 | tf_op jit(solution)/shard_map/while/body/eval_jaxpr/all_gather | solution.py:162
  828.8 55.9 %all-gather.7.cloned.1.call-start = ((), (), s32[]{:S(2)}) async-start(), calls=%async_computation.6 | async-start | bytes 3145728 | tf_op jit(solution)/shard_map/while/body/eval_jaxpr/all_gather | solution.py:76
  850.3 53.9 %reduce-scatter.5.cloned.1.call-start = ((), (), s32[]{:S(2)}) async-start(), calls=%async_computation.7 | async-start | bytes 786432 | tf_op jit(solution)/shard_map/while/body/eval_jaxpr/reduce_scatter | solution.py:84
  889.4 49.0 %reduce-scatter.7.cloned.1.call-start = ((), (), s32[]{:S(2)}) async-start(), calls=%async_computation.9 | async-start | bytes 3145728 | tf_op jit(solution)/shard_map/while/body/eval_jaxpr/reduce_scatter | solution.py:81
  901.4 62.5 %all-reduce.2.cloned.1.call-start = ((), (), s32[]{:S(2)}) async-start(), calls=%async_computation.8 | async-start | bytes 524288 | tf_op jit(solution)/shard_map/while/body/eval_jaxpr/psum | solution.py:94
  904.2 82.3 %reduce-scatter.9.cloned.1.call-start = ((), (), s32[]{:S(2)}) async-start(), calls=%async_computation.10 | async-start | bytes 1572864 | tf_op jit(solution)/shard_map/while/body/eval_jaxpr/reduce_scatter | solution.py:89
  938.4 74.4 %all-gather.9.cloned.1.call-start = ((), (), s32[]{:S(2)}) async-start(), calls=%async_computation.11 | async-start | bytes 1572864 | tf_op jit(solution)/shard_map/while/body/eval_jaxpr/all_gather | solution.py:138
  991.4 56.1 %all-gather.11.cloned.1.call-start = ((), (), s32[]{:S(2)}) async-start(), calls=%async_computation.12 | async-start | bytes 3145728 | tf_op jit(solution)/shard_map/while/body/eval_jaxpr/all_gather | solution.py:139
  1012.8 70.4 %reduce-scatter.11.cloned.1.call-start = ((), (), s32[]{:S(2)}) async-start(), calls=%async_computation.13 | async-start | bytes 1572864 | tf_op jit(solution)/shard_map/while/body/eval_jaxpr/reduce_scatter | solution.py:163
  1074.5 8.7 copy-start.2
  1084.6 15.3 %collective-permute-start = (bf16[128,2048]{1,0:T(8,128)(2,1)S(1)}, bf16[128,2048]{1,0:T(8,128)(2,1)S(1)}, u32[]{:S(2)}, u32[]{:S(2)}) collective-permute-start(bf16[128,2048]{1,0:T(8,128)(2,1)S(1)} %get-tuple-element.592), channel_id=1, source_target_pairs={{0,8},{8,16},{16,24},{1,9},{9,17},{17,25},{2,10},{10,18},{18,26},{... | collective-permute-start | bytes 1572872 | tf_op jit(solution)/shard_map/while/body/eval_jaxpr/ppermute | solution.py:16
  1099.8 0.8 copy-start.3
  1099.8 0.8 copy-start.1
Sparse Core Ops, SparseCore 0:
  14.9 11.7 all-gather.4
  35.8 34.2 all-gather.6
  74.9 14.6 reduce-scatter.4
  91.7 31.8 reduce-scatter.6
  125.7 23.2 all-reduce.1
  151.2 20.3 reduce-scatter.8
  176.6 21.2 all-gather.8
  199.4 33.0 all-gather.10
  260.8 7.4 reduce-scatter.10
  287.0 10.9 all-gather.4
  307.1 34.2 all-gather.6
  346.2 14.6 reduce-scatter.4
  363.1 31.8 reduce-scatter.6
  397.2 23.2 all-reduce.1
  422.6 20.3 reduce-scatter.8
  448.0 21.2 all-gather.8
  470.7 33.0 all-gather.10
  532.1 7.4 reduce-scatter.10
  558.6 10.9 all-gather.4
  578.7 34.2 all-gather.6
  617.7 14.6 reduce-scatter.4
  634.7 31.8 reduce-scatter.6
  668.9 23.2 all-reduce.1
  694.3 20.3 reduce-scatter.8
  719.7 21.2 all-gather.8
  742.4 33.0 all-gather.10
  803.8 7.4 reduce-scatter.10
  830.3 10.9 all-gather.4
  850.4 34.2 all-gather.6
  889.5 14.6 reduce-scatter.4
  906.4 31.8 reduce-scatter.6
  940.6 23.2 all-reduce.1
  966.1 20.3 reduce-scatter.8
  991.5 21.2 all-gather.8
  1014.3 33.0 all-gather.10
  1075.7 7.4 reduce-scatter.10
where the time goes:
time: 1110 us
  waiting for transfers between devices  778 us (70%)
  blocking collectives  124 us (11%)
  matrix products  118 us (11%)
  other arithmetic  44.3 us (4%)
  starting transfers between devices  16.1 us (1%)
  between operations  13.1 us (1%)
  local copies, waits for them, and re-layouts  11.5 us (1%)
    all_gather x4, waiting for transfers between devices, attention_layer(): lax.all_gather(every_token, 'gx', axis=1, tiled=True)  138 us
    all_gather x4, waiting for transfers between devices, attention_layer(): all_tokens = lax.all_gather(normed, 'gy', axis=0, tiled=True)  138 us
    reduce_scatter x4, waiting for transfers between devices, attention_layer(): lax.psum_scatter(query_part.astype(jnp.bfloat16), 'gy', scatter_dimension...  136 us
    psum x4, waiting for transfers between devices, attention_layer(): lax.psum(pair_local.astype(jnp.bfloat16), 'gx').astype(jnp.float32)  100 us
    all_gather x4, waiting for transfers between devices, attention_layer(): every_token = lax.all_gather(attended, 'gy', axis=0, tiled=True)  85.4 us
    all_to_all x4, blocking collectives, attention_layer(): lax.all_to_all(column_sums.astype(jnp.bfloat16), 'gy', split_axis=0, conc...  64.7 us
    all_gather x4, waiting for transfers between devices, advance(): wide_block = lax.all_gather(current, 'gz', axis=1, tiled=True)  50.1 us
    dot_general x4, matrix products, attention_layer(): jnp.dot(own_slab, query_weight, preferred_element_type=jnp.float32)  47.9 us
  transfers between devices with their start and end apart: 40, of which 40 were waited for; matrix products, arithmetic and copies ran while one was open for 5% of the time, Pallas kernels for 0%

commit v1 on v0

--- a/solution.py
+++ b/solution.py
@@ -73,7 +73,9 @@
         normed = (widened * lax.rsqrt(squares / D + EPSILON)[:, None] * gain_row[None, :]).astype(
             jnp.bfloat16
         )
-        all_tokens = lax.all_gather(normed, "gy", axis=0, tiled=True)
+        all_tokens = jnp.concatenate(
+            lax.all_to_all(jnp.stack([normed] * lax.axis_size("gy")), "gy", 0, 0), axis=0
+        )
         own_slab = lax.dynamic_slice_in_dim(all_tokens, index_gy * slab_rows, slab_rows, 1)
         query_part = jnp.dot(own_slab, query_weight, preferred_element_type=jnp.float32)
         pair_part = jnp.dot(own_slab, pair_weight, preferred_element_type=jnp.float32)

time: 1110 us -> 1070 us (0.964)
  waiting for transfers between devices: 778 us -> 640 us
  blocking collectives: 124 us -> 233 us
    all_gather x4 -> x0, waiting for transfers between devices: 138 us -> none  [attention_layer(): all_tokens = lax.all_gather(normed, 'gy', axis=0, tiled=True)]
    all_to_all x0 -> x4, blocking collectives: none -> 109 us  [attention_layer(): lax.all_to_all(jnp.stack([normed] * lax.axis_size('gy')), 'gy', 0, 0)]
  transfers between devices with their start and end apart: 40 -> 36, of which waited for: 40 -> 36; matrix products, arithmetic and copies ran while one was open for 5% -> 5% of each run, Pallas kernels for 0% -> 0%
where the time goes in v1:
time: 1070 us
  waiting for transfers between devices  640 us (60%)
  blocking collectives  233 us (22%)
  matrix products  107 us (10%)
  other arithmetic  45.2 us (4%)
  starting transfers between devices  16 us (1%)
  between operations  13.1 us (1%)
  local copies, waits for them, and re-layouts  11.5 us (1%)
    all_gather x4, waiting for transfers between devices, attention_layer(): lax.all_gather(every_token, 'gx', axis=1, tiled=True)  138 us
    reduce_scatter x4, waiting for transfers between devices, attention_layer(): lax.psum_scatter(query_part.astype(jnp.bfloat16), 'gy', scatter_dimension...  137 us
    all_to_all x4, blocking collectives, attention_layer(): lax.all_to_all(jnp.stack([normed] * lax.axis_size('gy')), 'gy', 0, 0)  109 us
    psum x4, waiting for transfers between devices, attention_layer(): lax.psum(pair_local.astype(jnp.bfloat16), 'gx').astype(jnp.float32)  100 us
    all_gather x4, waiting for transfers between devices, attention_layer(): every_token = lax.all_gather(attended, 'gy', axis=0, tiled=True)  85.4 us
    all_to_all x4, blocking collectives, attention_layer(): lax.all_to_all(column_sums.astype(jnp.bfloat16), 'gy', split_axis=0, conc...  64.7 us
    ppermute x4, waiting for transfers between devices, from_behind(): lax.ppermute(value, axis, [(source, source + steps) for source in range(i...  46.3 us
    dot_general x4, matrix products, attention_layer(): jnp.dot(own_slab, query_weight, preferred_element_type=jnp.float32)  46 us
  transfers between devices with their start and end apart: 36, of which 36 were waited for; matrix products, arithmetic and copies ran while one was open for 5% of the time, Pallas kernels for 0%

profile of v1, /device:TPU:0, one launch (start us, length us, event | category | flops | bytes accessed | tf_op | source)
XLA Modules:
  0.0 1066.7 jit_solution(6620930910813246326)
XLA Ops:
  12.5 1046.8 %while.19 = (s32[]{:T(128)}, bf16[128,2048]{1,0:T(8,128)(2,1)S(1)}, bf16[1,128,2048]{2,1,0:T(8,128)(2,1)S(1)}, pred[]{:T(512)}, bf16[1,128,2048]{2,1,0:T(8,128)(...) while((s32[]{:T(128)}, bf16[128,2048]{1,0:T(8,128)(2,1)S(1)}, ...), condition=%wide.region_10.11_spmd.clone.clone, body=%wide.region_0.10_spmd.clone.clone.sunk | while | flops 9951091712 | bytes 145197168 | solution.py:173
  14.5 12.1 %all-gather.4.cloned.1.call-done = bf16[128,4096]{1,0:T(8,128)(2,1)} async-done(((bf16[128,2048]{1,0:T(8,128)(2,1)}), bf16[128,4096]{1,0:T(8,128)(2,1)}) %all-gather.4.cloned.1.call-update) | async-done | bytes 1048592 | tf_op jit(solution)/shard_map/while/body/eval_jaxpr/all_gather | solution.py:164
  28.2 4.9 psum.34
  34.9 27.2 %all_to_all.63 = bf16[2,128,4096]{2,1,0:T(8,128)(2,1)S(1)} all-to-all(bf16[2,128,4096]{2,1,0:T(8,128)(2,1)S(1)} %pad_maximum_fusion.3), channel_id=1, replica_groups=mesh['section'=4,'gx'=2,'gy'=2,'gz'=2] {'gy'}, dimensions={0} | all-to-all | bytes 4194304 | tf_op jit(solution)/shard_map/while/body/eval_jaxpr/all_to_all | solution.py:77
  64.3 11.5 %convolution_convert_fusion.7 = bf16[256,4096]{1,0:T(8,128)(2,1)} fusion(bf16[2048,4096]{1,0:T(8,128)(2,1)} %get-tuple-element.638, bf16[256,4096]{1,0:T(8,128)(2,1)S(1)} %bitcast.145, s32[]{:T(128)} %get-tuple-element.634), kind=kOutput, calls=%fused_computation.2.clone.1 | convolution fusion | flops 4296015872 | bytes 19922948 | tf_op jit(solution)/shard_map/while/body/eval_jaxpr/dot_general | solution.py:80
  79.3 34.2 %reduce-scatter.7.cloned.1.call-done = bf16[128,4096]{1,0:T(8,128)(2,1)} async-done(((bf16[256,4096]{1,0:T(8,128)(2,1)}), bf16[128,4096]{1,0:T(8,128)(2,1)}) %reduce-scatter.7.cloned.1.call-update) | async-done | bytes 1048592 | tf_op jit(solution)/shard_map/while/body/eval_jaxpr/reduce_scatter | solution.py:83
  114.0 25.0 %all-reduce.2.cloned.1.call-done = bf16[128,1024]{1,0:T(8,128)(2,1)} async-done(((bf16[128,1024]{1,0:T(8,128)(2,1)}), bf16[128,1024]{1,0:T(8,128)(2,1)}) %all-reduce.2.cloned.1.call-update) | async-done | bytes 262160 | tf_op jit(solution)/shard_map/while/body/eval_jaxpr/psum | solution.py:96
  140.9 5.0 all_gather.67
  145.9 5.0 all_gather.66
  150.8 10.6 reduce-scatter.9.cloned.1.call-done
  166.4 21.4 %all-gather.6.cloned.1.call-done = bf16[256,2048]{0,1:T(8,128)(2,1)} async-done(((bf16[128,2048]{0,1:T(8,128)(2,1)}), bf16[256,2048]{0,1:T(8,128)(2,1)}) %all-gather.6.cloned.1.call-update) | async-done | bytes 1048592 | tf_op jit(solution)/shard_map/while/body/eval_jaxpr/all_gather | solution.py:140
  187.8 34.6 %all-gather.8.cloned.1.call-done = bf16[256,4096]{0,1:T(8,128)(2,1)} async-done(((bf16[256,2048]{0,1:T(8,128)(2,1)}), bf16[256,4096]{0,1:T(8,128)(2,1)}) %all-gather.8.cloned.1.call-update) | async-done | bytes 2097168 | tf_op jit(solution)/shard_map/while/body/eval_jaxpr/all_gather | solution.py:141
  222.4 10.9 %convolution_convert_fusion.8 = bf16[256,2048]{1,0:T(8,128)(2,1)S(1)} fusion(bf16[256,4096]{0,1:T(8,128)(2,1)} %all-gather.8.cloned.1.call-done, bf16[4096,2048]{1,0:T(8,128)(2,1)} %get-tuple-element.640), kind=kOutput, calls=%fused_computation.5.clone.1 | convolution fusion | flops 4295491584 | bytes 19922944 | tf_op jit(solution)/shard_map/while/body/eval_jaxpr/dot_general | solution.py:68
  233.3 16.2 %all_to_all.64 = bf16[2,128,2048]{2,1,0:T(8,128)(2,1)S(1)} all-to-all(bf16[2,128,2048]{2,1,0:T(8,128)(2,1)S(1)} %bitcast.139), channel_id=1, replica_groups=mesh['section'=4,'gx'=2,'gy'=2,'gz'=2] {'gy'}, dimensions={0} | all-to-all | bytes 2097152 | tf_op jit(solution)/shard_map/while/body/eval_jaxpr/all_to_all | solution.py:142
  250.6 7.6 reduce-scatter.11.cloned.1.call-done
  259.6 3.7 collective-permute-start
  263.3 11.6 %collective-permute-done = bf16[128,2048]{1,0:T(8,128)(2,1)S(1)} collective-permute-done((bf16[128,2048]{1,0:T(8,128)(2,1)S(1)}, bf16[128,2048]{1,0:T(8,128)(2,1)S(1)}, u32[]{:S(2)}, u32[]{:S(2)}) %collective-permute-start) | collective-permute-done | bytes 524320 | tf_op jit(solution)/shard_map/while/body/eval_jaxpr/ppermute | solution.py:16
  276.8 11.4 %all-gather.4.cloned.1.call-done = bf16[128,4096]{1,0:T(8,128)(2,1)} async-done(((bf16[128,2048]{1,0:T(8,128)(2,1)}), bf16[128,4096]{1,0:T(8,128)(2,1)}) %all-gather.4.cloned.1.call-update) | async-done | bytes 1048592 | tf_op jit(solution)/shard_map/while/body/eval_jaxpr/all_gather | solution.py:164
  289.7 4.9 psum.34
  296.4 27.2 %all_to_all.63 = bf16[2,128,4096]{2,1,0:T(8,128)(2,1)S(1)} all-to-all(bf16[2,128,4096]{2,1,0:T(8,128)(2,1)S(1)} %pad_maximum_fusion.3), channel_id=1, replica_groups=mesh['section'=4,'gx'=2,'gy'=2,'gz'=2] {'gy'}, dimensions={0} | all-to-all | bytes 4194304 | tf_op jit(solution)/shard_map/while/body/eval_jaxpr/all_to_all | solution.py:77
  325.8 11.5 %convolution_convert_fusion.7 = bf16[256,4096]{1,0:T(8,128)(2,1)} fusion(bf16[2048,4096]{1,0:T(8,128)(2,1)} %get-tuple-element.638, bf16[256,4096]{1,0:T(8,128)(2,1)S(1)} %bitcast.145, s32[]{:T(128)} %get-tuple-element.634), kind=kOutput, calls=%fused_computation.2.clone.1 | convolution fusion | flops 4296015872 | bytes 19922948 | tf_op jit(solution)/shard_map/while/body/eval_jaxpr/dot_general | solution.py:80
  340.8 34.2 %reduce-scatter.7.cloned.1.call-done = bf16[128,4096]{1,0:T(8,128)(2,1)} async-done(((bf16[256,4096]{1,0:T(8,128)(2,1)}), bf16[128,4096]{1,0:T(8,128)(2,1)}) %reduce-scatter.7.cloned.1.call-update) | async-done | bytes 1048592 | tf_op jit(solution)/shard_map/while/body/eval_jaxpr/reduce_scatter | solution.py:83
  375.5 25.0 %all-reduce.2.cloned.1.call-done = bf16[128,1024]{1,0:T(8,128)(2,1)} async-done(((bf16[128,1024]{1,0:T(8,128)(2,1)}), bf16[128,1024]{1,0:T(8,128)(2,1)}) %all-reduce.2.cloned.1.call-update) | async-done | bytes 262160 | tf_op jit(solution)/shard_map/while/body/eval_jaxpr/psum | solution.py:96
  402.4 5.0 all_gather.67
  407.4 5.0 all_gather.66
  412.3 10.8 %reduce-scatter.9.cloned.1.call-done = bf16[128,2048]{1,0:T(8,128)(2,1)} async-done(((bf16[128,4096]{1,0:T(8,128)(2,1)}), bf16[128,2048]{1,0:T(8,128)(2,1)}) %reduce-scatter.9.cloned.1.call-update) | async-done | bytes 524304 | tf_op jit(solution)/shard_map/while/body/eval_jaxpr/reduce_scatter | solution.py:91
  428.1 21.4 %all-gather.6.cloned.1.call-done = bf16[256,2048]{0,1:T(8,128)(2,1)} async-done(((bf16[128,2048]{0,1:T(8,128)(2,1)}), bf16[256,2048]{0,1:T(8,128)(2,1)}) %all-gather.6.cloned.1.call-update) | async-done | bytes 1048592 | tf_op jit(solution)/shard_map/while/body/eval_jaxpr/all_gather | solution.py:140
  449.5 34.4 %all-gather.8.cloned.1.call-done = bf16[256,4096]{0,1:T(8,128)(2,1)} async-done(((bf16[256,2048]{0,1:T(8,128)(2,1)}), bf16[256,4096]{0,1:T(8,128)(2,1)}) %all-gather.8.cloned.1.call-update) | async-done | bytes 2097168 | tf_op jit(solution)/shard_map/while/body/eval_jaxpr/all_gather | solution.py:141
  483.9 10.9 %convolution_convert_fusion.8 = bf16[256,2048]{1,0:T(8,128)(2,1)S(1)} fusion(bf16[256,4096]{0,1:T(8,128)(2,1)} %all-gather.8.cloned.1.call-done, bf16[4096,2048]{1,0:T(8,128)(2,1)} %get-tuple-element.640), kind=kOutput, calls=%fused_computation.5.clone.1 | convolution fusion | flops 4295491584 | bytes 19922944 | tf_op jit(solution)/shard_map/while/body/eval_jaxpr/dot_general | solution.py:68
  494.8 16.2 %all_to_all.64 = bf16[2,128,2048]{2,1,0:T(8,128)(2,1)S(1)} all-to-all(bf16[2,128,2048]{2,1,0:T(8,128)(2,1)S(1)} %bitcast.139), channel_id=1, replica_groups=mesh['section'=4,'gx'=2,'gy'=2,'gz'=2] {'gy'}, dimensions={0} | all-to-all | bytes 2097152 | tf_op jit(solution)/shard_map/while/body/eval_jaxpr/all_to_all | solution.py:142
  512.1 7.6 reduce-scatter.11.cloned.1.call-done
  521.1 3.7 collective-permute-start
  524.8 11.6 %collective-permute-done = bf16[128,2048]{1,0:T(8,128)(2,1)S(1)} collective-permute-done((bf16[128,2048]{1,0:T(8,128)(2,1)S(1)}, bf16[128,2048]{1,0:T(8,128)(2,1)S(1)}, u32[]{:S(2)}, u32[]{:S(2)}) %collective-permute-start) | collective-permute-done | bytes 524320 | tf_op jit(solution)/shard_map/while/body/eval_jaxpr/ppermute | solution.py:16
  538.3 11.1 %all-gather.4.cloned.1.call-done = bf16[128,4096]{1,0:T(8,128)(2,1)} async-done(((bf16[128,2048]{1,0:T(8,128)(2,1)}), bf16[128,4096]{1,0:T(8,128)(2,1)}) %all-gather.4.cloned.1.call-update) | async-done | bytes 1048592 | tf_op jit(solution)/shard_map/while/body/eval_jaxpr/all_gather | solution.py:164
  550.9 4.9 psum.34
  557.6 27.2 %all_to_all.63 = bf16[2,128,4096]{2,1,0:T(8,128)(2,1)S(1)} all-to-all(bf16[2,128,4096]{2,1,0:T(8,128)(2,1)S(1)} %pad_maximum_fusion.3), channel_id=1, replica_groups=mesh['section'=4,'gx'=2,'gy'=2,'gz'=2] {'gy'}, dimensions={0} | all-to-all | bytes 4194304 | tf_op jit(solution)/shard_map/while/body/eval_jaxpr/all_to_all | solution.py:77
  587.0 11.5 %convolution_convert_fusion.7 = bf16[256,4096]{1,0:T(8,128)(2,1)} fusion(bf16[2048,4096]{1,0:T(8,128)(2,1)} %get-tuple-element.638, bf16[256,4096]{1,0:T(8,128)(2,1)S(1)} %bitcast.145, s32[]{:T(128)} %get-tuple-element.634), kind=kOutput, calls=%fused_computation.2.clone.1 | convolution fusion | flops 4296015872 | bytes 19922948 | tf_op jit(solution)/shard_map/while/body/eval_jaxpr/dot_general | solution.py:80
  602.0 34.2 %reduce-scatter.7.cloned.1.call-done = bf16[128,4096]{1,0:T(8,128)(2,1)} async-done(((bf16[256,4096]{1,0:T(8,128)(2,1)}), bf16[128,4096]{1,0:T(8,128)(2,1)}) %reduce-scatter.7.cloned.1.call-update) | async-done | bytes 1048592 | tf_op jit(solution)/shard_map/while/body/eval_jaxpr/reduce_scatter | solution.py:83
  636.7 25.0 %all-reduce.2.cloned.1.call-done = bf16[128,1024]{1,0:T(8,128)(2,1)} async-done(((bf16[128,1024]{1,0:T(8,128)(2,1)}), bf16[128,1024]{1,0:T(8,128)(2,1)}) %all-reduce.2.cloned.1.call-update) | async-done | bytes 262160 | tf_op jit(solution)/shard_map/while/body/eval_jaxpr/psum | solution.py:96
  663.6 5.0 all_gather.67
  668.6 5.0 all_gather.66
  673.5 10.8 %reduce-scatter.9.cloned.1.call-done = bf16[128,2048]{1,0:T(8,128)(2,1)} async-done(((bf16[128,4096]{1,0:T(8,128)(2,1)}), bf16[128,2048]{1,0:T(8,128)(2,1)}) %reduce-scatter.9.cloned.1.call-update) | async-done | bytes 524304 | tf_op jit(solution)/shard_map/while/body/eval_jaxpr/reduce_scatter | solution.py:91
  689.2 21.4 %all-gather.6.cloned.1.call-done = bf16[256,2048]{0,1:T(8,128)(2,1)} async-done(((bf16[128,2048]{0,1:T(8,128)(2,1)}), bf16[256,2048]{0,1:T(8,128)(2,1)}) %all-gather.6.cloned.1.call-update) | async-done | bytes 1048592 | tf_op jit(solution)/shard_map/while/body/eval_jaxpr/all_gather | solution.py:140
  710.7 34.6 %all-gather.8.cloned.1.call-done = bf16[256,4096]{0,1:T(8,128)(2,1)} async-done(((bf16[256,2048]{0,1:T(8,128)(2,1)}), bf16[256,4096]{0,1:T(8,128)(2,1)}) %all-gather.8.cloned.1.call-update) | async-done | bytes 2097168 | tf_op jit(solution)/shard_map/while/body/eval_jaxpr/all_gather | solution.py:141
  745.3 10.9 %convolution_convert_fusion.8 = bf16[256,2048]{1,0:T(8,128)(2,1)S(1)} fusion(bf16[256,4096]{0,1:T(8,128)(2,1)} %all-gather.8.cloned.1.call-done, bf16[4096,2048]{1,0:T(8,128)(2,1)} %get-tuple-element.640), kind=kOutput, calls=%fused_computation.5.clone.1 | convolution fusion | flops 4295491584 | bytes 19922944 | tf_op jit(solution)/shard_map/while/body/eval_jaxpr/dot_general | solution.py:68
  756.2 16.2 %all_to_all.64 = bf16[2,128,2048]{2,1,0:T(8,128)(2,1)S(1)} all-to-all(bf16[2,128,2048]{2,1,0:T(8,128)(2,1)S(1)} %bitcast.139), channel_id=1, replica_groups=mesh['section'=4,'gx'=2,'gy'=2,'gz'=2] {'gy'}, dimensions={0} | all-to-all | bytes 2097152 | tf_op jit(solution)/shard_map/while/body/eval_jaxpr/all_to_all | solution.py:142
  773.4 7.6 reduce-scatter.11.cloned.1.call-done
  782.4 3.7 collective-permute-start
  786.1 11.6 %collective-permute-done = bf16[128,2048]{1,0:T(8,128)(2,1)S(1)} collective-permute-done((bf16[128,2048]{1,0:T(8,128)(2,1)S(1)}, bf16[128,2048]{1,0:T(8,128)(2,1)S(1)}, u32[]{:S(2)}, u32[]{:S(2)}) %collective-permute-start) | collective-permute-done | bytes 524320 | tf_op jit(solution)/shard_map/while/body/eval_jaxpr/ppermute | solution.py:16
  799.7 11.3 %all-gather.4.cloned.1.call-done = bf16[128,4096]{1,0:T(8,128)(2,1)} async-done(((bf16[128,2048]{1,0:T(8,128)(2,1)}), bf16[128,4096]{1,0:T(8,128)(2,1)}) %all-gather.4.cloned.1.call-update) | async-done | bytes 1048592 | tf_op jit(solution)/shard_map/while/body/eval_jaxpr/all_gather | solution.py:164
  812.5 4.9 psum.34
  819.2 27.2 %all_to_all.63 = bf16[2,128,4096]{2,1,0:T(8,128)(2,1)S(1)} all-to-all(bf16[2,128,4096]{2,1,0:T(8,128)(2,1)S(1)} %pad_maximum_fusion.3), channel_id=1, replica_groups=mesh['section'=4,'gx'=2,'gy'=2,'gz'=2] {'gy'}, dimensions={0} | all-to-all | bytes 4194304 | tf_op jit(solution)/shard_map/while/body/eval_jaxpr/all_to_all | solution.py:77
  848.6 11.5 %convolution_convert_fusion.7 = bf16[256,4096]{1,0:T(8,128)(2,1)} fusion(bf16[2048,4096]{1,0:T(8,128)(2,1)} %get-tuple-element.638, bf16[256,4096]{1,0:T(8,128)(2,1)S(1)} %bitcast.145, s32[]{:T(128)} %get-tuple-element.634), kind=kOutput, calls=%fused_computation.2.clone.1 | convolution fusion | flops 4296015872 | bytes 19922948 | tf_op jit(solution)/shard_map/while/body/eval_jaxpr/dot_general | solution.py:80
  863.7 34.0 %reduce-scatter.7.cloned.1.call-done = bf16[128,4096]{1,0:T(8,128)(2,1)} async-done(((bf16[256,4096]{1,0:T(8,128)(2,1)}), bf16[128,4096]{1,0:T(8,128)(2,1)}) %reduce-scatter.7.cloned.1.call-update) | async-done | bytes 1048592 | tf_op jit(solution)/shard_map/while/body/eval_jaxpr/reduce_scatter | solution.py:83
  898.2 25.1 %all-reduce.2.cloned.1.call-done = bf16[128,1024]{1,0:T(8,128)(2,1)} async-done(((bf16[128,1024]{1,0:T(8,128)(2,1)}), bf16[128,1024]{1,0:T(8,128)(2,1)}) %all-reduce.2.cloned.1.call-update) | async-done | bytes 262160 | tf_op jit(solution)/shard_map/while/body/eval_jaxpr/psum | solution.py:96
  925.3 5.0 all_gather.67
  930.2 5.0 all_gather.66
  935.2 10.8 %reduce-scatter.9.cloned.1.call-done = bf16[128,2048]{1,0:T(8,128)(2,1)} async-done(((bf16[128,4096]{1,0:T(8,128)(2,1)}), bf16[128,2048]{1,0:T(8,128)(2,1)}) %reduce-scatter.9.cloned.1.call-update) | async-done | bytes 524304 | tf_op jit(solution)/shard_map/while/body/eval_jaxpr/reduce_scatter | solution.py:91
  950.9 21.4 %all-gather.6.cloned.1.call-done = bf16[256,2048]{0,1:T(8,128)(2,1)} async-done(((bf16[128,2048]{0,1:T(8,128)(2,1)}), bf16[256,2048]{0,1:T(8,128)(2,1)}) %all-gather.6.cloned.1.call-update) | async-done | bytes 1048592 | tf_op jit(solution)/shard_map/while/body/eval_jaxpr/all_gather | solution.py:140
  972.3 34.6 %all-gather.8.cloned.1.call-done = bf16[256,4096]{0,1:T(8,128)(2,1)} async-done(((bf16[256,2048]{0,1:T(8,128)(2,1)}), bf16[256,4096]{0,1:T(8,128)(2,1)}) %all-gather.8.cloned.1.call-update) | async-done | bytes 2097168 | tf_op jit(solution)/shard_map/while/body/eval_jaxpr/all_gather | solution.py:141
  1006.9 10.9 %convolution_convert_fusion.8 = bf16[256,2048]{1,0:T(8,128)(2,1)S(1)} fusion(bf16[256,4096]{0,1:T(8,128)(2,1)} %all-gather.8.cloned.1.call-done, bf16[4096,2048]{1,0:T(8,128)(2,1)} %get-tuple-element.640), kind=kOutput, calls=%fused_computation.5.clone.1 | convolution fusion | flops 4295491584 | bytes 19922944 | tf_op jit(solution)/shard_map/while/body/eval_jaxpr/dot_general | solution.py:68
  1017.8 16.2 %all_to_all.64 = bf16[2,128,2048]{2,1,0:T(8,128)(2,1)S(1)} all-to-all(bf16[2,128,2048]{2,1,0:T(8,128)(2,1)S(1)} %bitcast.139), channel_id=1, replica_groups=mesh['section'=4,'gx'=2,'gy'=2,'gz'=2] {'gy'}, dimensions={0} | all-to-all | bytes 2097152 | tf_op jit(solution)/shard_map/while/body/eval_jaxpr/all_to_all | solution.py:142
  1035.1 7.6 reduce-scatter.11.cloned.1.call-done
  1047.8 11.6 %collective-permute-done = bf16[128,2048]{1,0:T(8,128)(2,1)S(1)} collective-permute-done((bf16[128,2048]{1,0:T(8,128)(2,1)S(1)}, bf16[128,2048]{1,0:T(8,128)(2,1)S(1)}, u32[]{:S(2)}, u32[]{:S(2)}) %collective-permute-start) | collective-permute-done | bytes 524320 | tf_op jit(solution)/shard_map/while/body/eval_jaxpr/ppermute | solution.py:16
  (224 shorter events, 92.7 us)
Async XLA Ops:
  6.5 0.7 copy-start
  9.8 2.7 copy-start.5
  9.8 2.7 copy-start.6
  12.5 14.1 %all-gather.4.cloned.1.call-start = ((), (), s32[]{:S(2)}) async-start(), calls=%async_computation.6 | async-start | bytes 1572864 | tf_op jit(solution)/shard_map/while/body/eval_jaxpr/all_gather | solution.py:164
  14.5 64.8 %reduce-scatter.5.cloned.1.call-start = ((), (), s32[]{:S(2)}) async-start(), calls=%async_computation.7 | async-start | bytes 786432 | tf_op jit(solution)/shard_map/while/body/eval_jaxpr/reduce_scatter | solution.py:86
  34.9 27.2 %copy-start.4 = (bf16[2048,1024]{1,0:T(8,128)(2,1)S(1)}, bf16[2048,1024]{1,0:T(8,128)(2,1)}, u32[]{:S(2)}) copy-start(bf16[2048,1024]{1,0:T(8,128)(2,1)} %get-tuple-element.635) | copy-start | bytes 12582916 | tf_op jit(solution)/shard_map/while
  64.2 49.3 %reduce-scatter.7.cloned.1.call-start = ((), (), s32[]{:S(2)}) async-start(), calls=%async_computation.9 | async-start | bytes 3145728 | tf_op jit(solution)/shard_map/while/body/eval_jaxpr/reduce_scatter | solution.py:83
  75.8 63.2 %all-reduce.2.cloned.1.call-start = ((), (), s32[]{:S(2)}) async-start(), calls=%async_computation.8 | async-start | bytes 524288 | tf_op jit(solution)/shard_map/while/body/eval_jaxpr/psum | solution.py:96
  79.3 82.2 %reduce-scatter.9.cloned.1.call-start = ((), (), s32[]{:S(2)}) async-start(), calls=%async_computation.10 | async-start | bytes 1572864 | tf_op jit(solution)/shard_map/while/body/eval_jaxpr/reduce_scatter | solution.py:91
  113.5 74.2 %all-gather.6.cloned.1.call-start = ((), (), s32[]{:S(2)}) async-start(), calls=%async_computation.11 | async-start | bytes 1572864 | tf_op jit(solution)/shard_map/while/body/eval_jaxpr/all_gather | solution.py:140
  166.4 56.1 %all-gather.8.cloned.1.call-start = ((), (), s32[]{:S(2)}) async-start(), calls=%async_computation.12 | async-start | bytes 3145728 | tf_op jit(solution)/shard_map/while/body/eval_jaxpr/all_gather | solution.py:141
  187.8 70.4 %reduce-scatter.11.cloned.1.call-start = ((), (), s32[]{:S(2)}) async-start(), calls=%async_computation.13 | async-start | bytes 1572864 | tf_op jit(solution)/shard_map/while/body/eval_jaxpr/reduce_scatter | solution.py:165
  249.5 8.7 copy-start.2
  259.6 15.3 %collective-permute-start = (bf16[128,2048]{1,0:T(8,128)(2,1)S(1)}, bf16[128,2048]{1,0:T(8,128)(2,1)S(1)}, u32[]{:S(2)}, u32[]{:S(2)}) collective-permute-start(bf16[128,2048]{1,0:T(8,128)(2,1)S(1)} %get-tuple-element.592), channel_id=1, source_target_pairs={{0,8},{8,16},{16,24},{1,9},{9,17},{17,25},{2,10},{10,18},{18,26},{... | collective-permute-start | bytes 1572872 | tf_op jit(solution)/shard_map/while/body/eval_jaxpr/ppermute | solution.py:16
  274.8 13.3 %all-gather.4.cloned.1.call-start = ((), (), s32[]{:S(2)}) async-start(), calls=%async_computation.6 | async-start | bytes 1572864 | tf_op jit(solution)/shard_map/while/body/eval_jaxpr/all_gather | solution.py:164
  276.8 64.0 %reduce-scatter.5.cloned.1.call-start = ((), (), s32[]{:S(2)}) async-start(), calls=%async_computation.7 | async-start | bytes 786432 | tf_op jit(solution)/shard_map/while/body/eval_jaxpr/reduce_scatter | solution.py:86
  296.4 27.2 %copy-start.4 = (bf16[2048,1024]{1,0:T(8,128)(2,1)S(1)}, bf16[2048,1024]{1,0:T(8,128)(2,1)}, u32[]{:S(2)}) copy-start(bf16[2048,1024]{1,0:T(8,128)(2,1)} %get-tuple-element.635) | copy-start | bytes 12582916 | tf_op jit(solution)/shard_map/while
  325.7 49.3 %reduce-scatter.7.cloned.1.call-start = ((), (), s32[]{:S(2)}) async-start(), calls=%async_computation.9 | async-start | bytes 3145728 | tf_op jit(solution)/shard_map/while/body/eval_jaxpr/reduce_scatter | solution.py:83
  337.3 63.2 %all-reduce.2.cloned.1.call-start = ((), (), s32[]{:S(2)}) async-start(), calls=%async_computation.8 | async-start | bytes 524288 | tf_op jit(solution)/shard_map/while/body/eval_jaxpr/psum | solution.py:96
  340.8 82.3 %reduce-scatter.9.cloned.1.call-start = ((), (), s32[]{:S(2)}) async-start(), calls=%async_computation.10 | async-start | bytes 1572864 | tf_op jit(solution)/shard_map/while/body/eval_jaxpr/reduce_scatter | solution.py:91
  375.0 74.4 %all-gather.6.cloned.1.call-start = ((), (), s32[]{:S(2)}) async-start(), calls=%async_computation.11 | async-start | bytes 1572864 | tf_op jit(solution)/shard_map/while/body/eval_jaxpr/all_gather | solution.py:140
  428.0 55.9 %all-gather.8.cloned.1.call-start = ((), (), s32[]{:S(2)}) async-start(), calls=%async_computation.12 | async-start | bytes 3145728 | tf_op jit(solution)/shard_map/while/body/eval_jaxpr/all_gather | solution.py:141
  449.4 70.3 %reduce-scatter.11.cloned.1.call-start = ((), (), s32[]{:S(2)}) async-start(), calls=%async_computation.13 | async-start | bytes 1572864 | tf_op jit(solution)/shard_map/while/body/eval_jaxpr/reduce_scatter | solution.py:165
  511.0 8.7 copy-start.2
  521.1 15.3 %collective-permute-start = (bf16[128,2048]{1,0:T(8,128)(2,1)S(1)}, bf16[128,2048]{1,0:T(8,128)(2,1)S(1)}, u32[]{:S(2)}, u32[]{:S(2)}) collective-permute-start(bf16[128,2048]{1,0:T(8,128)(2,1)S(1)} %get-tuple-element.592), channel_id=1, source_target_pairs={{0,8},{8,16},{16,24},{1,9},{9,17},{17,25},{2,10},{10,18},{18,26},{... | collective-permute-start | bytes 1572872 | tf_op jit(solution)/shard_map/while/body/eval_jaxpr/ppermute | solution.py:16
  536.3 13.0 %all-gather.4.cloned.1.call-start = ((), (), s32[]{:S(2)}) async-start(), calls=%async_computation.6 | async-start | bytes 1572864 | tf_op jit(solution)/shard_map/while/body/eval_jaxpr/all_gather | solution.py:164
  538.3 63.7 %reduce-scatter.5.cloned.1.call-start = ((), (), s32[]{:S(2)}) async-start(), calls=%async_computation.7 | async-start | bytes 786432 | tf_op jit(solution)/shard_map/while/body/eval_jaxpr/reduce_scatter | solution.py:86
  557.6 27.2 %copy-start.4 = (bf16[2048,1024]{1,0:T(8,128)(2,1)S(1)}, bf16[2048,1024]{1,0:T(8,128)(2,1)}, u32[]{:S(2)}) copy-start(bf16[2048,1024]{1,0:T(8,128)(2,1)} %get-tuple-element.635) | copy-start | bytes 12582916 | tf_op jit(solution)/shard_map/while
  586.9 49.3 %reduce-scatter.7.cloned.1.call-start = ((), (), s32[]{:S(2)}) async-start(), calls=%async_computation.9 | async-start | bytes 3145728 | tf_op jit(solution)/shard_map/while/body/eval_jaxpr/reduce_scatter | solution.py:83
  598.5 63.1 %all-reduce.2.cloned.1.call-start = ((), (), s32[]{:S(2)}) async-start(), calls=%async_computation.8 | async-start | bytes 524288 | tf_op jit(solution)/shard_map/while/body/eval_jaxpr/psum | solution.py:96
  602.0 82.3 %reduce-scatter.9.cloned.1.call-start = ((), (), s32[]{:S(2)}) async-start(), calls=%async_computation.10 | async-start | bytes 1572864 | tf_op jit(solution)/shard_map/while/body/eval_jaxpr/reduce_scatter | solution.py:91
  636.2 74.4 %all-gather.6.cloned.1.call-start = ((), (), s32[]{:S(2)}) async-start(), calls=%async_computation.11 | async-start | bytes 1572864 | tf_op jit(solution)/shard_map/while/body/eval_jaxpr/all_gather | solution.py:140
  689.2 56.1 %all-gather.8.cloned.1.call-start = ((), (), s32[]{:S(2)}) async-start(), calls=%async_computation.12 | async-start | bytes 3145728 | tf_op jit(solution)/shard_map/while/body/eval_jaxpr/all_gather | solution.py:141
  710.6 70.4 %reduce-scatter.11.cloned.1.call-start = ((), (), s32[]{:S(2)}) async-start(), calls=%async_computation.13 | async-start | bytes 1572864 | tf_op jit(solution)/shard_map/while/body/eval_jaxpr/reduce_scatter | solution.py:165
  772.4 8.7 copy-start.2
  782.4 15.3 %collective-permute-start = (bf16[128,2048]{1,0:T(8,128)(2,1)S(1)}, bf16[128,2048]{1,0:T(8,128)(2,1)S(1)}, u32[]{:S(2)}, u32[]{:S(2)}) collective-permute-start(bf16[128,2048]{1,0:T(8,128)(2,1)S(1)} %get-tuple-element.592), channel_id=1, source_target_pairs={{0,8},{8,16},{16,24},{1,9},{9,17},{17,25},{2,10},{10,18},{18,26},{... | collective-permute-start | bytes 1572872 | tf_op jit(solution)/shard_map/while/body/eval_jaxpr/ppermute | solution.py:16
  797.7 13.3 %all-gather.4.cloned.1.call-start = ((), (), s32[]{:S(2)}) async-start(), calls=%async_computation.6 | async-start | bytes 1572864 | tf_op jit(solution)/shard_map/while/body/eval_jaxpr/all_gather | solution.py:164
  799.6 64.0 %reduce-scatter.5.cloned.1.call-start = ((), (), s32[]{:S(2)}) async-start(), calls=%async_computation.7 | async-start | bytes 786432 | tf_op jit(solution)/shard_map/while/body/eval_jaxpr/reduce_scatter | solution.py:86
  819.2 27.2 %copy-start.4 = (bf16[2048,1024]{1,0:T(8,128)(2,1)S(1)}, bf16[2048,1024]{1,0:T(8,128)(2,1)}, u32[]{:S(2)}) copy-start(bf16[2048,1024]{1,0:T(8,128)(2,1)} %get-tuple-element.635) | copy-start | bytes 12582916 | tf_op jit(solution)/shard_map/while
  848.6 49.1 %reduce-scatter.7.cloned.1.call-start = ((), (), s32[]{:S(2)}) async-start(), calls=%async_computation.9 | async-start | bytes 3145728 | tf_op jit(solution)/shard_map/while/body/eval_jaxpr/reduce_scatter | solution.py:83
  860.2 63.1 %all-reduce.2.cloned.1.call-start = ((), (), s32[]{:S(2)}) async-start(), calls=%async_computation.8 | async-start | bytes 524288 | tf_op jit(solution)/shard_map/while/body/eval_jaxpr/psum | solution.py:96
  863.7 82.3 %reduce-scatter.9.cloned.1.call-start = ((), (), s32[]{:S(2)}) async-start(), calls=%async_computation.10 | async-start | bytes 1572864 | tf_op jit(solution)/shard_map/while/body/eval_jaxpr/reduce_scatter | solution.py:91
  897.7 74.6 %all-gather.6.cloned.1.call-start = ((), (), s32[]{:S(2)}) async-start(), calls=%async_computation.11 | async-start | bytes 1572864 | tf_op jit(solution)/shard_map/while/body/eval_jaxpr/all_gather | solution.py:140
  950.9 56.1 %all-gather.8.cloned.1.call-start = ((), (), s32[]{:S(2)}) async-start(), calls=%async_computation.12 | async-start | bytes 3145728 | tf_op jit(solution)/shard_map/while/body/eval_jaxpr/all_gather | solution.py:141
  972.3 70.4 %reduce-scatter.11.cloned.1.call-start = ((), (), s32[]{:S(2)}) async-start(), calls=%async_computation.13 | async-start | bytes 1572864 | tf_op jit(solution)/shard_map/while/body/eval_jaxpr/reduce_scatter | solution.py:165
  1034.0 8.7 copy-start.2
  1044.1 15.3 %collective-permute-start = (bf16[128,2048]{1,0:T(8,128)(2,1)S(1)}, bf16[128,2048]{1,0:T(8,128)(2,1)S(1)}, u32[]{:S(2)}, u32[]{:S(2)}) collective-permute-start(bf16[128,2048]{1,0:T(8,128)(2,1)S(1)} %get-tuple-element.592), channel_id=1, source_target_pairs={{0,8},{8,16},{16,24},{1,9},{9,17},{17,25},{2,10},{10,18},{18,26},{... | collective-permute-start | bytes 1572872 | tf_op jit(solution)/shard_map/while/body/eval_jaxpr/ppermute | solution.py:16
  1059.3 0.8 copy-start.3
  1059.3 0.8 copy-start.1
Sparse Core Ops, SparseCore 0:
  14.9 11.7 all-gather.3
  64.3 14.8 reduce-scatter.4
  81.5 31.9 reduce-scatter.6
  115.6 23.2 all-reduce.1
  141.1 20.3 reduce-scatter.8
  166.5 21.2 all-gather.5
  189.3 33.0 all-gather.7
  250.7 7.4 reduce-scatter.10
  277.2 10.9 all-gather.3
  325.8 14.8 reduce-scatter.4
  343.0 31.9 reduce-scatter.6
  377.1 23.2 all-reduce.1
  402.7 20.3 reduce-scatter.8
  428.1 21.2 all-gather.5
  450.8 33.0 all-gather.7
  512.2 7.4 reduce-scatter.10
  538.4 10.9 all-gather.3
  587.0 14.8 reduce-scatter.4
  604.2 31.9 reduce-scatter.6
  638.3 23.2 all-reduce.1
  663.9 20.3 reduce-scatter.8
  689.3 21.2 all-gather.5
  712.2 33.0 all-gather.7
  773.5 7.4 reduce-scatter.10
  800.1 10.9 all-gather.3
  848.7 14.8 reduce-scatter.4
  865.7 31.9 reduce-scatter.6
  900.0 23.2 all-reduce.1
  925.5 20.3 reduce-scatter.8
  951.0 21.2 all-gather.5
  973.8 33.0 all-gather.7
  1035.2 7.4 reduce-scatter.10
